TPU v7x, 32 devices: a 4x2x2 block of a 4x4x8 slice. The times are simulated.
32 devices in a mesh: dp: 4 (over y, z), ep: 8 (over x, core).
Axes of the slice: x: 4, y: 2, z: 2, core: 2. Of those that a mesh axis runs over, the one named last changes fastest.
The devices are a block of a 4x4x8 slice.
Arguments:
- hidden: bfloat16 [4096, 2304], P(('dp', 'ep')), parts along dimension 0
- expert_ids: int32 [4096, 2], P(('dp', 'ep')), parts along dimension 0
- norm_gain: bfloat16 [2304], replicated
- w_router: bfloat16 [2304, 8], replicated
- w_gate: bfloat16 [8, 2304, 5760], P('ep')
- w_up: bfloat16 [8, 2304, 5760], P('ep')
- w_down: bfloat16 [8, 5760, 2304], P('ep')
Outputs:
- output: bfloat16 [4096, 2304], P(('dp', 'ep')), parts along dimension 0
There are 4 independent parts. A program takes and returns all parts, laid end to end along the dimension named above; an argument that names none is the same for every part.
All inputs are finite; a program needn't handle non-finite values.
Results may differ from a plain program's by a relative error of at most 0.001.
Values are sent between devices in bfloat16 or wider.
A program may use at most 768 MiB of HBM per device.

v0:
```python
import jax
import jax.numpy as jnp
from jax import lax
from jax.sharding import PartitionSpec as P

NORM_EPS = 1e-5


def rms_norm(hidden, norm_gain):
    hidden_f32 = hidden.astype(jnp.float32)
    mean_sq = jnp.mean(hidden_f32 * hidden_f32, axis=-1, keepdims=True)
    return (hidden_f32 * lax.rsqrt(mean_sq + NORM_EPS) * norm_gain.astype(jnp.float32)).astype(jnp.bfloat16)


def route_gates(normed, expert_ids, w_router):
    logits = jnp.dot(normed, w_router, preferred_element_type=jnp.float32)
    hit_mask = expert_ids[:, :, None] == jnp.arange(w_router.shape[1])[None, None, :]
    picked = jnp.sum(jnp.where(hit_mask, logits[:, None, :], 0.0), axis=-1)
    return jax.nn.softmax(picked, axis=-1)


def slot_positions(expert_ids, experts):
    tok_rows = expert_ids.shape[0]
    slot_order = jnp.concatenate([expert_ids[:, 0], expert_ids[:, 1]])
    hit_table = (slot_order[:, None] == jnp.arange(experts)[None, :]).astype(jnp.int32)
    seen_before = jnp.cumsum(hit_table, axis=0) - hit_table
    slot_rank = jnp.sum(seen_before * hit_table, axis=1)
    return slot_rank.reshape(2, tok_rows).T


def solution(mesh):
    token_spec = P(("dp", "ep"), None)
    expert_spec = P("ep", None, None)

    def local_block(hidden, expert_ids, norm_gain, w_router, w_gate, w_up, w_down):
        tok_rows, model_width = hidden.shape
        experts = w_router.shape[1]
        local_experts = w_gate.shape[0]
        group_size = experts // local_experts
        capacity = (5 * tok_rows + 2 * experts - 1) // (2 * experts)
        normed = rms_norm(hidden, norm_gain)
        gate_probs = route_gates(normed, expert_ids, w_router)
        positions = slot_positions(expert_ids, experts)
        expert_grid = jnp.arange(group_size)[None, :] * local_experts + jnp.arange(local_experts)[:, None]
        select = ((expert_ids[:, :, None, None, None] == expert_grid[:, :, None])
                  & (positions[:, :, None, None, None] == jnp.arange(capacity))).astype(jnp.bfloat16)
        send_buf = jnp.einsum("tslgc,td->lgcd", select, normed, preferred_element_type=jnp.float32).astype(jnp.bfloat16)
        send_buf = send_buf.reshape(local_experts, group_size * capacity, model_width)
        recv_buf = lax.all_to_all(send_buf, "ep", 1, 1, tiled=True)
        gate_proj = jnp.einsum("emd,edf->emf", recv_buf, w_gate, preferred_element_type=jnp.float32)
        up_proj = jnp.einsum("emd,edf->emf", recv_buf, w_up, preferred_element_type=jnp.float32)
        hidden_act = (jax.nn.silu(gate_proj) * up_proj).astype(jnp.bfloat16)
        expert_out = jnp.einsum("emf,efd->emd", hidden_act, w_down, preferred_element_type=jnp.float32).astype(jnp.bfloat16)
        back_buf = lax.all_to_all(expert_out, "ep", 1, 1, tiled=True)
        back_buf = back_buf.reshape(local_experts, group_size, capacity, model_width)
        fetched = jnp.einsum("tslgc,lgcd->tsd", select, back_buf, preferred_element_type=jnp.float32)
        mixed_sum = jnp.sum(gate_probs[:, :, None] * fetched, axis=1)
        return (hidden.astype(jnp.float32) + mixed_sum).astype(jnp.bfloat16)

    return jax.shard_map(local_block, mesh=mesh,
                         in_specs=(token_spec, token_spec, P(None), P(None, None), expert_spec, expert_spec, expert_spec),
                         out_specs=token_spec, check_vma=False)
```

profile of v0, /device:TPU:81, one launch (start us, length us, event | category | flops | bytes accessed | tf_op | source)
XLA Modules:
  0.0 150.0 jit_solution(12439347547101964669)
XLA Ops:
  0.0 0.0 copy-start
  0.0 0.8 slice_bitcast_fusion.1
  0.8 0.7 iota_compare_fusion.3
  1.4 1.3 fusion.32
  2.7 0.6 reduce-window.6
  3.3 0.2 slice_reduce_fusion
  3.6 0.1 fusion.47
  3.7 0.7 convert_element_type.57
  4.4 1.7 %convolution_convert_fusion = bf16[8,40,2304]{2,1,0:T(8,128)(2,1)S(1)} fusion(bf16[128,8,40]{0,2,1:T(8,128)(2,1)S(1)} %convert_reduce_fusion, bf16[128,2304]{1,0:T(8,128)(2,1)} %param.7, f32[2304]{0:T(1024)S(1)} %convert_element_type.57, f32[128]{0:T(128)S(1)} %add_rsqrt_fusion), kind=kOutput, calls=%fused_computation.12 | convolution fusion | flops 189923328 | bytes 2156032 | tf_op jit(solution)/shard_map/tslgc,td->lgcd/dot_general | solution.py:47
  6.1 2.3 %copy.37 = bf16[1,320,2304]{2,0,1:T(2,128)(2,1)S(1)} copy(bf16[1,320,2304]{2,1,0:T(8,128)(2,1)S(1)} %bitcast.74) | data formatting | bytes 2949120 | tf_op jit(solution)/shard_map/reshape | solution.py:48
  8.4 0.5 broadcast.104
  8.9 11.3 %reduce.3 = bf16[320,2304]{1,0:T(8,128)(2,1)} reduce(bf16[320,1,2304]{2,1,0:T(2,128)(2,1)S(1)} %bitcast.71, bf16[]{:T(256)} %broadcast.104), dimensions={1}, to_apply=%bitcast.70.reduce_sub_computation | reduce | bytes 2949122
  20.2 2.3 %reshape.152 = bf16[8,2,46080]{2,1,0:T(2,128)(2,1)S(1)} reshape(bf16[320,2304]{1,0:T(8,128)(2,1)} %reduce.3) | data formatting | bytes 2949120
  22.6 25.4 %all_to_all.10 = bf16[8,2,46080]{2,1,0:T(2,128)(2,1)S(1)} all-to-all(bf16[8,2,46080]{2,1,0:T(2,128)(2,1)S(1)} %reshape.152), channel_id=1, replica_groups=mesh['dp'=4,'ep'=8] {'ep'}, dimensions={0} | all-to-all | bytes 2949120 | tf_op jit(solution)/shard_map/all_to_all | solution.py:49
  48.0 3.8 %reshape.153 = bf16[320,1,2304]{2,1,0:T(2,128)(2,1)} reshape(bf16[8,2,46080]{2,1,0:T(2,128)(2,1)S(1)} %all_to_all.10) | data formatting | bytes 2949120
  51.7 0.0 copy-start.3
  51.7 20.7 %fusion.4 = f32[320,5760]{1,0:T(8,128)} fusion(bf16[1,2304,5760]{2,1,0:T(8,128)(2,1)} %param.11, bf16[1,320,2304]{2,0,1:T(2,128)(2,1)} %bitcast.75), kind=kOutput, calls=%fused_computation.4 | convolution fusion | flops 8493465600 | bytes 35389440 | tf_op jit(solution)/shard_map/emd,edf->emf/dot_general | solution.py:50
  72.4 0.0 copy-done.3
  72.4 27.7 %fusion.22 = bf16[1,320,2304]{2,1,0:T(8,128)(2,1)} fusion(bf16[1,5760,2304]{2,1,0:T(8,128)(2,1)} %param.13, bf16[1,2304,5760]{2,1,0:T(8,128)(2,1)} %param.12, f32[320,5760]{1,0:T(8,128)} %fusion.4, bf16[1,320,2304]{2,0,1:T(2,128)(2,1)S(1)} %bitcast.76), kind=kOutput, calls=%fused_computation.14 | convolution fusion | flops 16998727680 | bytes 63406080 | tf_op jit(solution)/shard_map/emf,efd->emd/dot_general | solution.py:53
  100.2 3.6 %copy.36 = bf16[1,320,2304]{2,0,1:T(2,128)(2,1)S(1)} copy(bf16[1,320,2304]{2,1,0:T(8,128)(2,1)} %fusion.22) | data formatting | bytes 2949120 | tf_op jit(solution)/shard_map/convert_element_type | solution.py:53
  103.8 11.1 %reduce.4 = bf16[320,2304]{1,0:T(8,128)(2,1)} reduce(bf16[320,1,2304]{2,1,0:T(2,128)(2,1)S(1)} %bitcast.72, bf16[]{:T(256)} %broadcast.104), dimensions={1}, to_apply=%bitcast.69.reduce_sub_computation | reduce | bytes 2949122
  114.9 0.0 copy-start.1
  114.9 3.7 %reshape.154 = bf16[8,2,46080]{2,1,0:T(2,128)(2,1)} reshape(bf16[320,2304]{1,0:T(8,128)(2,1)} %reduce.4) | data formatting | bytes 2949120
  118.6 0.0 copy-start.4
  118.7 5.2 %all-to-all-start.1 = ((bf16[8,2,46080]{2,1,0:T(2,128)(2,1)}), bf16[8,2,46080]{2,1,0:T(2,128)(2,1)}, u32[]{:S(2)}, u32[]{:S(2)}) async-start(bf16[8,2,46080]{2,1,0:T(2,128)(2,1)} %reshape.154), calls=%async_computation.1 | async-start | bytes 2949120 | tf_op jit(solution)/shard_map/all_to_all | solution.py:54
  123.9 0.0 copy-done
  123.9 0.0 copy-done.1
  123.9 0.3 fusion.42
  124.2 0.0 copy-done.4
  124.2 0.1 select_reduce_fusion
  124.3 19.1 %all-to-all-done.1 = bf16[8,2,46080]{2,1,0:T(2,128)(2,1)} async-done(((bf16[8,2,46080]{2,1,0:T(2,128)(2,1)}), bf16[8,2,46080]{2,1,0:T(2,128)(2,1)}, u32[]{:S(2)}, u32[]{:S(2)}) %all-to-all-start.1) | async-done | bytes 1474592 | tf_op jit(solution)/shard_map/all_to_all | solution.py:54
  143.4 4.5 %reshape.155 = bf16[320,1,2304]{2,1,0:T(2,128)(2,1)S(1)} reshape(bf16[8,2,46080]{2,1,0:T(2,128)(2,1)} %all-to-all-done.1) | data formatting | bytes 2949120
  147.9 0.2 copy.24
  148.0 0.0 copy-start.2
  148.0 0.8 fusion.28
  148.9 0.2 copy-done.2
  149.1 0.9 fusion.35
  (10 shorter events, 0.2 us)
Async XLA Ops:
  0.0 123.9 %copy-start = (bf16[2304,8]{0,1:T(8,128)(2,1)S(1)}, bf16[2304,8]{0,1:T(8,128)(2,1)}, u32[]{:S(2)}) copy-start(bf16[2304,8]{0,1:T(8,128)(2,1)} %param.10) | copy-start | bytes 110596
  51.7 20.7 %copy-start.3 = (bf16[320,1,2304]{2,1,0:T(2,128)(2,1)S(1)}, bf16[320,1,2304]{2,1,0:T(2,128)(2,1)}, u32[]{:S(2)}) copy-start(bf16[320,1,2304]{2,1,0:T(2,128)(2,1)} %reshape.153) | copy-start | bytes 4423684
  114.9 8.9 %copy-start.1 = (bf16[128,2304]{1,0:T(8,128)(2,1)S(1)}, bf16[128,2304]{1,0:T(8,128)(2,1)}, u32[]{:S(2)}) copy-start(bf16[128,2304]{1,0:T(8,128)(2,1)} %param.7) | copy-start | bytes 1769476
  118.6 5.5 %copy-start.4 = (s32[128,2]{0,1:T(2,128)S(1)}, s32[128,2]{0,1:T(2,128)}, u32[]{:S(2)}) copy-start(s32[128,2]{0,1:T(2,128)} %param.8) | copy-start | bytes 3076
  118.7 24.7 %all-to-all-start.1 = ((bf16[8,2,46080]{2,1,0:T(2,128)(2,1)}), bf16[8,2,46080]{2,1,0:T(2,128)(2,1)}, u32[]{:S(2)}, u32[]{:S(2)}) async-start(bf16[8,2,46080]{2,1,0:T(2,128)(2,1)} %reshape.154), calls=%async_computation.1 | async-start | bytes 2949120 | tf_op jit(solution)/shard_map/all_to_all | solution.py:54
  148.0 1.1 copy-start.2
where the time goes:
time: 151 us; the launch traced here: 150 us
  matrix products  51.2 us (34%)
  other arithmetic  26.9 us (18%)
  blocking collectives  25.4 us (17%)
  local copies, waits for them, and re-layouts  22.1 us (15%)
  waiting for transfers between devices  19.1 us (13%)
  starting transfers between devices  5.21 us (3%)
    dot_general x1, matrix products, local_block(): jnp.einsum('emf,efd->emd', hidden_act, w_down, preferred_element_type=jnp...  27.7 us
    all_to_all x1, blocking collectives, local_block(): recv_buf = lax.all_to_all(send_buf, 'ep', 1, 1, tiled=True)  25.4 us
    unnamed x2, other arithmetic  22.4 us
    dot_general x1, matrix products, local_block(): jnp.einsum('emd,edf->emf', recv_buf, w_gate, preferred_element_type=jnp.f...  20.7 us
    all_to_all x1, waiting for transfers between devices, local_block(): back_buf = lax.all_to_all(expert_out, 'ep', 1, 1, tiled=True)  19.1 us
    unnamed x16, local copies, waits for them, and re-layouts  15.2 us
    all_to_all x1, starting transfers between devices, local_block(): back_buf = lax.all_to_all(expert_out, 'ep', 1, 1, tiled=True)  5.21 us
    convert_element_type x1, local copies, waits for them, and re-layouts, local_block(): jnp.einsum('emf,efd->emd', hidden_act, w_down, preferred_element_type=jnp...  3.65 us
  transfers between devices with their start and end apart: 1, of which 1 were waited for; matrix products, arithmetic and copies ran while one was open for 0% of the time, Pallas kernels for 0%

commit v1 on v0

v1 whole, which is shorter than its diff:
```python
import functools

import jax
import jax.numpy as jnp
from jax import lax
from jax.experimental import pallas as pl
from jax.experimental.pallas import tpu as pltpu
from jax.sharding import PartitionSpec as P

NORM_EPS = 1e-5
CHIPS = 4
BLOCKS = 8
FCOLS = 640
NCOLS = 256
K_CHUNKS = (256, 512, 512, 512, 512)
WD_SLOTS = 3


def block_pairs():
    return [(d, s) for d in (2, 1, 3, 0) for s in (0, 1) if (d, s) != (0, 0)]


def moe_kernel(cap, x_hbm, ids_hbm, gain_hbm, router_hbm, wg_hbm, wu_hbm, wd_hbm, out_hbm,
               x_v, ids_v, gain_v, router_v, u_v, w_ring, wd_ring, acc, h_v, u2_v, o_stage, back, out_v, *rest):
    nk = len(K_CHUNKS)
    stage = rest[:nk]
    recv = rest[nk:2 * nk]
    in_sem, w_sem, wd_sem, ds_sem, dr_sem, os_sem, or_sem, out_sem = rest[2 * nk:]
    rows, width = x_v.shape
    ff = h_v.shape[1]
    slots = BLOCKS * cap
    n_f = ff // FCOLS
    n_n = width // NCOLS
    k_off = [sum(K_CHUNKS[:i]) for i in range(nk)]

    me = lax.axis_index("ep")
    chip = me // 2
    core = me % 2

    def peer(d, s):
        return {"ep": lax.rem(chip + d, CHIPS) * 2 + lax.rem(core + s, 2)}

    in_copies = [pltpu.make_async_copy(a, b, in_sem.at[i]) for i, (a, b) in enumerate(
        ((x_hbm, x_v), (ids_hbm, ids_v), (gain_hbm, gain_v), (router_hbm, router_v)))]
    for cp in in_copies:
        cp.start()

    def w_copies(kc, f):
        slot = (kc % 2) * n_f + f
        rows_k = pl.ds(k_off[kc], K_CHUNKS[kc])
        cols = pl.ds(pl.multiple_of(f * FCOLS, 128), FCOLS)
        dst = w_ring.at[slot, pl.ds(0, K_CHUNKS[kc])]
        return (pltpu.make_async_copy(wg_hbm.at[0, rows_k, cols], dst.at[:, pl.ds(0, FCOLS)], w_sem.at[slot, 0]),
                pltpu.make_async_copy(wu_hbm.at[0, rows_k, cols], dst.at[:, pl.ds(FCOLS, FCOLS)], w_sem.at[slot, 1]))

    def wd_copy(n, slot):
        cols = pl.ds(pl.multiple_of(n * NCOLS, 128), NCOLS)
        return pltpu.make_async_copy(wd_hbm.at[0, :, cols], wd_ring.at[slot], wd_sem.at[slot])

    barrier = pltpu.get_barrier_semaphore()
    for d, s in block_pairs():
        pl.semaphore_signal(barrier, inc=1, device_id=peer(d, s))

    for kc in range(2):
        @pl.loop(0, n_f)
        def _(f):
            for cp in w_copies(kc, f):
                cp.start()

    for cp in in_copies:
        cp.wait()

    xf = x_v[...].astype(jnp.float32)
    mean_sq = jnp.sum(xf * xf, axis=-1, keepdims=True) * (1.0 / width)
    u = (xf * lax.rsqrt(mean_sq + NORM_EPS) * gain_v[...].astype(jnp.float32)).astype(jnp.bfloat16)
    u_v[...] = u

    ids0 = ids_v[:, 0:1]
    ids1 = ids_v[:, 1:2]
    lane = lax.broadcasted_iota(jnp.int32, (rows, 128), 1)
    hit0 = jnp.where(lane == ids0, 1.0, 0.0).astype(jnp.float32)
    hit1 = jnp.where(lane == ids1 + BLOCKS, 1.0, 0.0).astype(jnp.float32)
    before = jnp.where(lax.broadcasted_iota(jnp.int32, (rows, rows), 0) > lax.broadcasted_iota(jnp.int32, (rows, rows), 1),
                       1.0, 0.0).astype(jnp.bfloat16)
    seen = jnp.dot(before, (hit0 + hit1).astype(jnp.bfloat16), preferred_element_type=jnp.float32)
    total0 = jnp.sum(hit0, axis=0, keepdims=True)
    pos0 = jnp.sum(seen * hit0, axis=1, keepdims=True)
    pos1 = jnp.sum(seen * hit1 + jnp.where(lane == ids1, total0, 0.0), axis=1, keepdims=True)

    def slot_of(ids, pos):
        block = ((((ids >> 1) - chip) & (CHIPS - 1)) << 1) | ((ids & 1) ^ core)
        return jnp.where(pos < cap, (block * cap).astype(jnp.float32) + pos, -1.0)

    slot0 = slot_of(ids0, pos0)
    slot1 = slot_of(ids1, pos1)
    slot_iota = lax.broadcasted_iota(jnp.int32, (rows, 384), 1).astype(jnp.float32)
    take0 = jnp.where(slot_iota == slot0, 1.0, 0.0)
    take1 = jnp.where(slot_iota == slot1, 1.0, 0.0)
    pick = jnp.transpose(take0 + take1)[:slots].astype(jnp.bfloat16)

    def dispatch(kc, wait_barrier):
        cols = pl.ds(k_off[kc], K_CHUNKS[kc])
        part = jnp.dot(pick, u_v[:, cols], preferred_element_type=jnp.float32).astype(jnp.bfloat16)
        stage[kc][pl.ds(0, slots), :] = part
        recv[kc][pl.ds(0, cap), :] = part[:cap]
        if wait_barrier:
            pl.semaphore_wait(barrier, BLOCKS - 1)
        for d, s in block_pairs():
            send_copy(kc, d, s).start()

    def send_copy(kc, d, s):
        b = d * 2 + s
        rb = ((CHIPS - d) % CHIPS) * 2 + s
        return pltpu.make_async_remote_copy(
            src_ref=stage[kc].at[pl.ds(b * cap, cap)], dst_ref=recv[kc].at[pl.ds(rb * cap, cap)],
            send_sem=ds_sem.at[kc, b], recv_sem=dr_sem.at[kc, rb], device_id=peer(d, s))

    for kc in range(nk):
        dispatch(kc, kc == 0)

    logits = jnp.dot(u, router_v[...], preferred_element_type=jnp.float32)
    lane8 = lax.broadcasted_iota(jnp.int32, logits.shape, 1)
    pick0 = jnp.sum(jnp.where(lane8 == ids0, logits, 0.0), axis=1, keepdims=True)
    pick1 = jnp.sum(jnp.where(lane8 == ids1, logits, 0.0), axis=1, keepdims=True)
    top = jnp.maximum(pick0, pick1)
    e0 = jnp.exp(pick0 - top)
    e1 = jnp.exp(pick1 - top)
    gate0 = e0 / (e0 + e1)
    gate1 = e1 / (e0 + e1)
    fetch = jnp.concatenate([take0[:, :slots], take1[:, :slots]], axis=0).astype(jnp.bfloat16)

    for kc in range(nk):
        size = K_CHUNKS[kc]
        for d, s in block_pairs():
            send_copy(kc, d, s).wait_recv()
        u2_v[:, pl.ds(0, size)] = recv[kc][pl.ds(0, slots), :]

        @pl.loop(0, n_f)
        def _(f):
            for cp in w_copies(kc, f):
                cp.wait()
            slot = (kc % 2) * n_f + f
            prod = jnp.dot(u2_v[:, pl.ds(0, size)], w_ring[slot, pl.ds(0, size)], preferred_element_type=jnp.float32)
            if kc == 0:
                acc[f] = prod
            elif kc < nk - 1:
                acc[f] = acc[f] + prod
            else:
                g = acc[f, :, pl.ds(0, FCOLS)] + prod[:, :FCOLS]
                v = acc[f, :, pl.ds(FCOLS, FCOLS)] + prod[:, FCOLS:]
                h_v[:, pl.ds(pl.multiple_of(f * FCOLS, 128), FCOLS)] = (jax.nn.silu(g) * v).astype(jnp.bfloat16)
            if kc + 2 < nk:
                for cp in w_copies(kc + 2, f):
                    cp.start()

        if kc == nk - 3:
            for n in range(WD_SLOTS):
                wd_copy(n, n).start()

    def back_copy(n, r, s):
        b = r * 2 + s
        rb = ((CHIPS - r) % CHIPS) * 2 + s
        return pltpu.make_async_remote_copy(
            src_ref=o_stage.at[n, pl.ds(b * cap, cap)], dst_ref=back.at[n, pl.ds(rb * cap, cap)],
            send_sem=os_sem.at[n, b], recv_sem=or_sem.at[n, rb], device_id=peer(r, s))

    @pl.loop(0, n_n)
    def _(n):
        slot = lax.rem(n, WD_SLOTS)
        wd_copy(n, slot).wait()
        o = jnp.dot(h_v[...], wd_ring[slot], preferred_element_type=jnp.float32).astype(jnp.bfloat16)
        o_stage[n, pl.ds(0, slots)] = o
        back[n, pl.ds(0, cap)] = o[:cap]
        for r, s in block_pairs():
            back_copy(n, r, s).start()

        @pl.when(n + WD_SLOTS < n_n)
        def _():
            wd_copy(n + WD_SLOTS, slot).start()

    def out_copy(n):
        cols = pl.ds(pl.multiple_of(n * NCOLS, 128), NCOLS)
        return pltpu.make_async_copy(out_v.at[:, cols], out_hbm.at[:, cols], out_sem.at[n])

    @pl.loop(0, n_n)
    def _(n):
        for r, s in block_pairs():
            back_copy(n, r, s).wait_recv()
        got = jnp.dot(fetch, back[n, pl.ds(0, slots)], preferred_element_type=jnp.float32)
        cols = pl.ds(pl.multiple_of(n * NCOLS, 128), NCOLS)
        y = gate0 * got[:rows] + gate1 * got[rows:]
        out_v[:, cols] = (x_v[:, cols].astype(jnp.float32) + y).astype(jnp.bfloat16)
        out_copy(n).start()

    for kc in range(nk):
        for d, s in block_pairs():
            send_copy(kc, d, s).wait_send()

    @pl.loop(0, n_n)
    def _(n):
        for r, s in block_pairs():
            back_copy(n, r, s).wait_send()
        out_copy(n).wait()


def solution(mesh):
    token_spec = P(("dp", "ep"), None)
    expert_spec = P("ep", None, None)

    def local_block(hidden, expert_ids, norm_gain, w_router, w_gate, w_up, w_down):
        rows, width = hidden.shape
        ff = w_gate.shape[2]
        experts = w_router.shape[1]
        cap = (5 * rows + 2 * experts - 1) // (2 * experts)
        slots = BLOCKS * cap
        padded = slots + 8
        n_f = ff // FCOLS
        n_n = width // NCOLS
        nk = len(K_CHUNKS)
        bf16, f32 = jnp.bfloat16, jnp.float32
        dma = pltpu.SemaphoreType.DMA
        hbm = pl.BlockSpec(memory_space=pl.ANY)
        return pl.pallas_call(
            functools.partial(moe_kernel, cap),
            out_shape=jax.ShapeDtypeStruct((rows, width), bf16),
            in_specs=[hbm] * 7,
            out_specs=hbm,
            scratch_shapes=[
                pltpu.VMEM((rows, width), bf16),
                pltpu.VMEM(expert_ids.shape, jnp.int32),
                pltpu.VMEM((1, width), bf16),
                pltpu.VMEM(w_router.shape, bf16),
                pltpu.VMEM((rows, width), bf16),
                pltpu.VMEM((2 * n_f, max(K_CHUNKS), 2 * FCOLS), bf16),
                pltpu.VMEM((WD_SLOTS, ff, NCOLS), bf16),
                pltpu.VMEM((n_f, slots, 2 * FCOLS), f32),
                pltpu.VMEM((slots, ff), bf16),
                pltpu.VMEM((slots, max(K_CHUNKS)), bf16),
                pltpu.VMEM((n_n, padded, NCOLS), bf16),
                pltpu.VMEM((n_n, padded, NCOLS), bf16),
                pltpu.VMEM((rows, width), bf16),
                *[pltpu.VMEM((padded, k), bf16) for k in K_CHUNKS],
                *[pltpu.VMEM((padded, k), bf16) for k in K_CHUNKS],
                dma((4,)),
                dma((2 * n_f, 2)),
                dma((WD_SLOTS,)),
                dma((nk, BLOCKS)),
                dma((nk, BLOCKS)),
                dma((n_n, BLOCKS)),
                dma((n_n, BLOCKS)),
                dma((n_n,)),
            ],
            compiler_params=pltpu.CompilerParams(collective_id=0, has_side_effects=True, vmem_limit_bytes=67043328),
        )(hidden, expert_ids, norm_gain.reshape(1, width), w_router, w_gate, w_up, w_down)

    return jax.shard_map(local_block, mesh=mesh,
                         in_specs=(token_spec, token_spec, P(None), P(None, None), expert_spec, expert_spec, expert_spec),
                         out_specs=token_spec, check_vma=False)
```

time: 151 us -> 64.3 us (0.43)
  Pallas kernels: 0 us -> 57.6 us
  matrix products: 51.2 us -> 0 us
  other arithmetic: 26.9 us -> 0 us
  blocking collectives: 25.4 us -> 0 us
  waiting for transfers between devices: 19.1 us -> 0 us
  local copies, waits for them, and re-layouts: 22.1 us -> 6.43 us
  starting transfers between devices: 5.21 us -> 0 us
    pallas_call x0 -> x1, Pallas kernels: none -> 57.6 us  [local_block(): pl.pallas_call(functools.partial(moe_kernel, cap), out_shape=jax.ShapeDty...]
    dot_general x5 -> x0, matrix products: 51.2 us -> none  [the longest x1 27.7 us: local_block(): jnp.einsum('emf,efd->emd', hidden_act, w_down, preferred_element_type=jnp...]
    all_to_all x1 -> x0, blocking collectives: 25.4 us -> none  [local_block(): recv_buf = lax.all_to_all(send_buf, 'ep', 1, 1, tiled=True)]
    unnamed x2 -> x0, other arithmetic: 22.4 us -> none
    all_to_all x1 -> x0, waiting for transfers between devices: 19.1 us -> none  [local_block(): back_buf = lax.all_to_all(expert_out, 'ep', 1, 1, tiled=True)]
    unnamed x16 -> x3, local copies, waits for them, and re-layouts: 15.2 us -> 5.14 us
    all_to_all x1 -> x0, starting transfers between devices: 5.21 us -> none  [local_block(): back_buf = lax.all_to_all(expert_out, 'ep', 1, 1, tiled=True)]
    convert_element_type x1 -> x0, local copies, waits for them, and re-layouts: 3.65 us -> none  [local_block(): jnp.einsum('emf,efd->emd', hidden_act, w_down, preferred_element_type=jnp...]
  transfers between devices with their start and end apart: 1 -> 0, of which waited for: 1 -> 0; matrix products, arithmetic and copies ran while one was open for 0% -> 0% of each run, Pallas kernels for 0% -> 0%
where the time goes in v1:
time: 64.3 us; the launch traced here: 64 us
  Pallas kernels  57.6 us (90%)
  local copies, waits for them, and re-layouts  6.43 us (10%)
    pallas_call x1, Pallas kernels, local_block(): pl.pallas_call(functools.partial(moe_kernel, cap), out_shape=jax.ShapeDty...  57.6 us
    unnamed x3, local copies, waits for them, and re-layouts  5.14 us
    reshape x1, local copies, waits for them, and re-layouts, local_block(): norm_gain.reshape(1, width)  1.29 us

profile of v1, /device:TPU:81, one launch (start us, length us, event | category | flops | bytes accessed | tf_op | source)
XLA Modules:
  0.0 64.0 jit_solution(13789497542901867578)
XLA Ops:
  0.0 1.3 %reshape.3.gain_hbm = bf16[1,2304]{1,0:T(2,128)(2,1)} reshape(bf16[2304]{0:T(1024)(128)(2,1)} %param.9) | data formatting | bytes 9216 | tf_op jit(solution)/shard_map/reshape | solution.py:254
  1.3 1.4 %copy.8.ids_hbm = s32[128,2]{1,0:T(8,128)} copy(s32[128,2]{0,1:T(2,128)} %param.8) | data formatting | bytes 2048 | tf_op args[1]
  2.7 1.8 %copy.9.router_hbm = bf16[2304,8]{1,0:T(8,128)(2,1)} copy(bf16[2304,8]{0,1:T(8,128)(2,1)} %param.10) | data formatting | bytes 73728 | tf_op args[3]
  4.5 57.6 %shard_map.73 = bf16[128,2304]{1,0:T(8,128)(2,1)} custom-call(bf16[128,2304]{1,0:T(8,128)(2,1)} %x_hbm.1, s32[128,2]{1,0:T(8,128)} %copy.8.ids_hbm, bf16[1,2304]{1,0:T(2,128)(2,1)} %reshape.3.gain_hbm, bf16[2304,8]{1,0:T(8,128)(2,1)} %copy.9.router_hbm, bf16[1,2304,5760]{2,1,0:T(8,128)(2,1)} %wg_hbm.1, bf16[1,2304,5760]{2,1,0:T(8,128)(2,1)} %wu_hbm.1, ...), custom_call_target="tpu_custom_call" | custom-call | tf_op jit(solution)/shard_map/pallas_call | solution.py:223
  62.1 1.9 %copy.11 = bf16[128,2304]{1,0:T(8,128)(2,1)} copy(bf16[128,2304]{1,0:T(8,128)(2,1)} %shard_map.73) | data formatting | bytes 1179648

commit v2 on v1

--- a/solution.py
+++ b/solution.py
@@ -10,7 +10,7 @@
 NORM_EPS = 1e-5
 CHIPS = 4
 BLOCKS = 8
-FCOLS = 640
+FCOLS = 1920
 NCOLS = 256
 K_CHUNKS = (256, 512, 512, 512, 512)
 WD_SLOTS = 3
@@ -20,12 +20,12 @@
     return [(d, s) for d in (2, 1, 3, 0) for s in (0, 1) if (d, s) != (0, 0)]
 
 
-def moe_kernel(cap, x_hbm, ids_hbm, gain_hbm, router_hbm, wg_hbm, wu_hbm, wd_hbm, out_hbm,
-               x_v, ids_v, gain_v, router_v, u_v, w_ring, wd_ring, acc, h_v, u2_v, o_stage, back, out_v, *rest):
+def moe_kernel(cap, x_hbm, ids_hbm, gain_hbm, router_hbm, wg_hbm, wu_hbm, wd_hbm, out_ref,
+               x_v, ids_v, gain_v, router_v, u_v, w_ring, wd_ring, acc, h_v, u2_v, o_stage, back, *rest):
     nk = len(K_CHUNKS)
     stage = rest[:nk]
     recv = rest[nk:2 * nk]
-    in_sem, w_sem, wd_sem, ds_sem, dr_sem, os_sem, or_sem, out_sem = rest[2 * nk:]
+    in_sem, w_sem, wd_sem, ds_sem, dr_sem, os_sem, or_sem = rest[2 * nk:]
     rows, width = x_v.shape
     ff = h_v.shape[1]
     slots = BLOCKS * cap
@@ -45,13 +45,18 @@
     for cp in in_copies:
         cp.start()
 
+    remote = pl.ds(cap, slots - cap)
+
+    def wait_bytes(ref, sem):
+        pltpu.make_async_copy(ref, ref, sem).wait()
+
     def w_copies(kc, f):
         slot = (kc % 2) * n_f + f
         rows_k = pl.ds(k_off[kc], K_CHUNKS[kc])
         cols = pl.ds(pl.multiple_of(f * FCOLS, 128), FCOLS)
         dst = w_ring.at[slot, pl.ds(0, K_CHUNKS[kc])]
-        return (pltpu.make_async_copy(wg_hbm.at[0, rows_k, cols], dst.at[:, pl.ds(0, FCOLS)], w_sem.at[slot, 0]),
-                pltpu.make_async_copy(wu_hbm.at[0, rows_k, cols], dst.at[:, pl.ds(FCOLS, FCOLS)], w_sem.at[slot, 1]))
+        return (pltpu.make_async_copy(wg_hbm.at[0, rows_k, cols], dst.at[:, pl.ds(0, FCOLS)], w_sem.at[slot]),
+                pltpu.make_async_copy(wu_hbm.at[0, rows_k, cols], dst.at[:, pl.ds(FCOLS, FCOLS)], w_sem.at[slot]))
 
     def wd_copy(n, slot):
         cols = pl.ds(pl.multiple_of(n * NCOLS, 128), NCOLS)
@@ -67,16 +72,18 @@
             for cp in w_copies(kc, f):
                 cp.start()
 
-    for cp in in_copies:
-        cp.wait()
+    with jax.named_scope('in_wait'):
+        for cp in in_copies:
+            cp.wait()
 
     xf = x_v[...].astype(jnp.float32)
     mean_sq = jnp.sum(xf * xf, axis=-1, keepdims=True) * (1.0 / width)
-    u = (xf * lax.rsqrt(mean_sq + NORM_EPS) * gain_v[...].astype(jnp.float32)).astype(jnp.bfloat16)
+    u = (xf * lax.rsqrt(mean_sq + NORM_EPS) * gain_v[...].reshape(1, width).astype(jnp.float32)).astype(jnp.bfloat16)
     u_v[...] = u
 
-    ids0 = ids_v[:, 0:1]
-    ids1 = ids_v[:, 1:2]
+    ids_t = jnp.transpose(jnp.broadcast_to(ids_v[...].astype(jnp.float32)[:, None, :], (2, 8, rows)).reshape(16, rows))
+    ids0 = ids_t[:, 0:1].astype(jnp.int32)
+    ids1 = ids_t[:, 8:9].astype(jnp.int32)
     lane = lax.broadcasted_iota(jnp.int32, (rows, 128), 1)
     hit0 = jnp.where(lane == ids0, 1.0, 0.0).astype(jnp.float32)
     hit1 = jnp.where(lane == ids1 + BLOCKS, 1.0, 0.0).astype(jnp.float32)
@@ -113,12 +120,13 @@
         rb = ((CHIPS - d) % CHIPS) * 2 + s
         return pltpu.make_async_remote_copy(
             src_ref=stage[kc].at[pl.ds(b * cap, cap)], dst_ref=recv[kc].at[pl.ds(rb * cap, cap)],
-            send_sem=ds_sem.at[kc, b], recv_sem=dr_sem.at[kc, rb], device_id=peer(d, s))
+            send_sem=ds_sem.at[kc], recv_sem=dr_sem.at[kc], device_id=peer(d, s))
 
     for kc in range(nk):
-        dispatch(kc, kc == 0)
-
-    logits = jnp.dot(u, router_v[...], preferred_element_type=jnp.float32)
+        with jax.named_scope(f'dispatch{kc}'):
+            dispatch(kc, kc == 0)
+
+    logits = lax.dot_general(u, router_v[...], (((1,), (1,)), ((), ())), preferred_element_type=jnp.float32)
     lane8 = lax.broadcasted_iota(jnp.int32, logits.shape, 1)
     pick0 = jnp.sum(jnp.where(lane8 == ids0, logits, 0.0), axis=1, keepdims=True)
     pick1 = jnp.sum(jnp.where(lane8 == ids1, logits, 0.0), axis=1, keepdims=True)
@@ -131,15 +139,15 @@
 
     for kc in range(nk):
         size = K_CHUNKS[kc]
-        for d, s in block_pairs():
-            send_copy(kc, d, s).wait_recv()
+        with jax.named_scope(f"recv{kc}"):
+            wait_bytes(recv[kc].at[remote], dr_sem.at[kc])
         u2_v[:, pl.ds(0, size)] = recv[kc][pl.ds(0, slots), :]
 
         @pl.loop(0, n_f)
         def _(f):
-            for cp in w_copies(kc, f):
-                cp.wait()
             slot = (kc % 2) * n_f + f
+            with jax.named_scope(f"weights{kc}"):
+                wait_bytes(w_ring.at[slot, pl.ds(0, size)], w_sem.at[slot])
             prod = jnp.dot(u2_v[:, pl.ds(0, size)], w_ring[slot, pl.ds(0, size)], preferred_element_type=jnp.float32)
             if kc == 0:
                 acc[f] = prod
@@ -162,12 +170,13 @@
         rb = ((CHIPS - r) % CHIPS) * 2 + s
         return pltpu.make_async_remote_copy(
             src_ref=o_stage.at[n, pl.ds(b * cap, cap)], dst_ref=back.at[n, pl.ds(rb * cap, cap)],
-            send_sem=os_sem.at[n, b], recv_sem=or_sem.at[n, rb], device_id=peer(r, s))
+            send_sem=os_sem.at[n], recv_sem=or_sem.at[n], device_id=peer(r, s))
 
     @pl.loop(0, n_n)
     def _(n):
         slot = lax.rem(n, WD_SLOTS)
-        wd_copy(n, slot).wait()
+        with jax.named_scope('wd'):
+            wd_copy(n, slot).wait()
         o = jnp.dot(h_v[...], wd_ring[slot], preferred_element_type=jnp.float32).astype(jnp.bfloat16)
         o_stage[n, pl.ds(0, slots)] = o
         back[n, pl.ds(0, cap)] = o[:cap]
@@ -178,29 +187,21 @@
         def _():
             wd_copy(n + WD_SLOTS, slot).start()
 
-    def out_copy(n):
-        cols = pl.ds(pl.multiple_of(n * NCOLS, 128), NCOLS)
-        return pltpu.make_async_copy(out_v.at[:, cols], out_hbm.at[:, cols], out_sem.at[n])
-
     @pl.loop(0, n_n)
     def _(n):
-        for r, s in block_pairs():
-            back_copy(n, r, s).wait_recv()
+        with jax.named_scope("back_recv"):
+            wait_bytes(back.at[n, remote], or_sem.at[n])
         got = jnp.dot(fetch, back[n, pl.ds(0, slots)], preferred_element_type=jnp.float32)
         cols = pl.ds(pl.multiple_of(n * NCOLS, 128), NCOLS)
         y = gate0 * got[:rows] + gate1 * got[rows:]
-        out_v[:, cols] = (x_v[:, cols].astype(jnp.float32) + y).astype(jnp.bfloat16)
-        out_copy(n).start()
+        out_ref[:, cols] = (x_v[:, cols].astype(jnp.float32) + y).astype(jnp.bfloat16)
 
     for kc in range(nk):
-        for d, s in block_pairs():
-            send_copy(kc, d, s).wait_send()
+        wait_bytes(stage[kc].at[remote], ds_sem.at[kc])
 
     @pl.loop(0, n_n)
     def _(n):
-        for r, s in block_pairs():
-            back_copy(n, r, s).wait_send()
-        out_copy(n).wait()
+        wait_bytes(o_stage.at[n, remote], os_sem.at[n])
 
 
 def solution(mesh):
@@ -222,14 +223,14 @@
         hbm = pl.BlockSpec(memory_space=pl.ANY)
         return pl.pallas_call(
             functools.partial(moe_kernel, cap),
-            out_shape=jax.ShapeDtypeStruct((rows, width), bf16),
+            out_shape=pltpu.VMEM((rows, width), bf16),
             in_specs=[hbm] * 7,
-            out_specs=hbm,
+            out_specs=pl.BlockSpec(memory_space=pltpu.VMEM),
             scratch_shapes=[
                 pltpu.VMEM((rows, width), bf16),
-                pltpu.VMEM(expert_ids.shape, jnp.int32),
-                pltpu.VMEM((1, width), bf16),
-                pltpu.VMEM(w_router.shape, bf16),
+                pltpu.VMEM(expert_ids.shape[::-1], jnp.int32),
+                pltpu.VMEM((width,), bf16),
+                pltpu.VMEM(w_router.shape[::-1], bf16),
                 pltpu.VMEM((rows, width), bf16),
                 pltpu.VMEM((2 * n_f, max(K_CHUNKS), 2 * FCOLS), bf16),
                 pltpu.VMEM((WD_SLOTS, ff, NCOLS), bf16),
@@ -238,20 +239,18 @@
                 pltpu.VMEM((slots, max(K_CHUNKS)), bf16),
                 pltpu.VMEM((n_n, padded, NCOLS), bf16),
                 pltpu.VMEM((n_n, padded, NCOLS), bf16),
-                pltpu.VMEM((rows, width), bf16),
                 *[pltpu.VMEM((padded, k), bf16) for k in K_CHUNKS],
                 *[pltpu.VMEM((padded, k), bf16) for k in K_CHUNKS],
                 dma((4,)),
-                dma((2 * n_f, 2)),
+                dma((2 * n_f,)),
                 dma((WD_SLOTS,)),
-                dma((nk, BLOCKS)),
-                dma((nk, BLOCKS)),
-                dma((n_n, BLOCKS)),
-                dma((n_n, BLOCKS)),
+                dma((nk,)),
+                dma((nk,)),
+                dma((n_n,)),
                 dma((n_n,)),
             ],
-            compiler_params=pltpu.CompilerParams(collective_id=0, has_side_effects=True, vmem_limit_bytes=67043328),
-        )(hidden, expert_ids, norm_gain.reshape(1, width), w_router, w_gate, w_up, w_down)
+            compiler_params=pltpu.CompilerParams(collective_id=0, has_side_effects=True, vmem_limit_bytes=64 * 1024 * 1000),
+        )(hidden, expert_ids.T, norm_gain, w_router.T, w_gate, w_up, w_down)
 
     return jax.shard_map(local_block, mesh=mesh,
                          in_specs=(token_spec, token_spec, P(None), P(None, None), expert_spec, expert_spec, expert_spec),

time: 64.3 us -> 51.8 us (0.81)
  Pallas kernels: 57.6 us -> 50.9 us
  local copies, waits for them, and re-layouts: 6.43 us -> 0.82 us
    pallas_call x1, Pallas kernels: 57.6 us -> 50.9 us  [local_block(): pl.pallas_call(functools.partial(moe_kernel, cap), out_shape=pltpu.VMEM((...]
    unnamed x3 -> x1, local copies, waits for them, and re-layouts: 5.14 us -> 0.82 us
    reshape x1 -> x0, local copies, waits for them, and re-layouts: 1.29 us -> none  [local_block(): norm_gain.reshape(1, width)]
where the time goes in v2:
time: 51.8 us; the launch traced here: 51.7 us
  Pallas kernels  50.9 us (98%)
  local copies, waits for them, and re-layouts  0.82 us (2%)
    pallas_call x1, Pallas kernels, local_block(): pl.pallas_call(functools.partial(moe_kernel, cap), out_shape=pltpu.VMEM((...  50.9 us

profile of v2, /device:TPU:81, one launch (start us, length us, event | category | flops | bytes accessed | tf_op | source)
XLA Modules:
  0.0 51.7 jit_solution(10367720984821136438)
XLA Ops:
  0.0 50.9 %shard_map.73 = bf16[128,2304]{1,0:T(8,128)(2,1)S(1)} custom-call(bf16[128,2304]{1,0:T(8,128)(2,1)} %x_hbm.1, s32[2,128]{1,0:T(2,128)} %bitcast.3, bf16[2304]{0:T(1024)(128)(2,1)} %gain_hbm.1, bf16[8,2304]{1,0:T(8,128)(2,1)} %bitcast.2, bf16[1,2304,5760]{2,1,0:T(8,128)(2,1)} %wg_hbm.1, bf16[1,2304,5760]{2,1,0:T(8,128)(2,1)} %wu_hbm.1, ...), custom_call_target="tpu_custom_call" | custom-call | tf_op jit(solution)/shard_map/pallas_call | solution.py:224
  50.9 0.8 %copy.9 = bf16[128,2304]{1,0:T(8,128)(2,1)} copy(bf16[128,2304]{1,0:T(8,128)(2,1)S(1)} %shard_map.73) | data formatting | bytes 1179648
